TPU v7x, 32 devices: a whole 2x2x4 slice. The times are simulated.
32 devices in a mesh: dp: 8 (over y, x, core), tensor: 4 (over z).
Axes of the slice: x: 2, y: 2, z: 4, core: 2. Of those that a mesh axis runs over, the one named last changes fastest.
Arguments:
- layer_input: bfloat16 [16384, 4096], P('dp', 'tensor'), may hold values from -54 to 54
- queries: bfloat16 [16384, 2048], P('dp', 'tensor'), may hold values from -6 to 6
- keys_values: bfloat16 [16384, 2, 1024], P('dp', None, 'tensor'), may hold values from -6 to 6
- out_grads: bfloat16 [16384, 2048], P('dp', 'tensor'), may hold values from -6 to 6
- log_sums: bfloat16 [16384, 16], P('dp', 'tensor'), may hold values from 2.5 to 5.5
- deltas: bfloat16 [16384, 16], P('dp', 'tensor'), may hold values from -1.5 to 1.5
- tile_fill: int32 [8, 16], replicated, may hold values from 1 to 128, as said below
- tile_cont: int32 [8, 16], replicated, may hold values from 0 to 1, as said below
- moment_first: float32 [4096, 2, 1024], P(('tensor', 'dp')), may hold values from -2 to 2
- moment_second: float32 [2, 8], replicated, may hold values from 0.05 to 0.5
Outputs:
- update: float32 [4096, 2, 1024], P(('tensor', 'dp'))
- new_first: float32 [4096, 2, 1024], P(('tensor', 'dp'))
- new_second: float32 [2, 8], replicated
Inputs may be any that keep to these rules, and one draw needn't show every extreme that they name: `tile_fill`: a tile followed by a tile with tile_cont 1 has all 128 positions live. Documents span one or two tiles: tile_cont is 0 for the first tile of each group and never 1 for two tiles in a row.
All inputs are finite; a program needn't handle non-finite values.
Results may differ from a plain program's by a relative error of at most 0.0055.
Values may be sent and summed in bfloat16 or wider, within the bound.
A program may use at most 64 MiB of HBM per device.

v0:
```python
import math

import jax
import jax.numpy as jnp
from jax import lax
from jax.sharding import PartitionSpec as P

D = 4096
HD = 128


ADAM_ONE = 0.9
ADAM_TWO = 0.95
ADAM_EPS = 1e-08


def band_grads(q_tiles, k_tiles, v_tiles, do_tiles, lse_tiles, delta_tiles, fill_tiles, cont_tiles):
    tile_total, block_len, groups, head_width = q_tiles.shape
    scale_qk = head_width ** (-0.5)
    zero_tile = jnp.zeros_like(k_tiles[:1])
    k_window = jnp.concatenate([jnp.concatenate([zero_tile, k_tiles[:-1]], 0), k_tiles], 1)
    v_window = jnp.concatenate([jnp.concatenate([zero_tile, v_tiles[:-1]], 0), v_tiles], 1)
    places = jnp.arange(block_len)
    live_rows = places[None, :] < fill_tiles[:, None]
    causal = places[:, None] >= places[None, :]
    own_part = live_rows[:, :, None] & causal[None]
    prev_part = (
        live_rows[:, :, None] & (cont_tiles[:, None, None] == 1) & (places[None, None, :] >= 0)
    )
    allowed = jnp.concatenate([prev_part, own_part], 2)[:, None]
    scores = (
        jnp.einsum("sqgd,skd->sgqk", q_tiles, k_window, preferred_element_type=jnp.float32)
        * scale_qk
    )
    lse_rows = jnp.swapaxes(lse_tiles.astype(jnp.float32), 1, 2)[..., None]
    delta_rows = jnp.swapaxes(delta_tiles.astype(jnp.float32), 1, 2)[..., None]
    prob_vals = jnp.where(allowed, jnp.exp(scores - lse_rows), 0.0)
    dprobs = jnp.einsum("sqgd,skd->sgqk", do_tiles, v_window, preferred_element_type=jnp.float32)
    dscores = prob_vals * (dprobs - delta_rows)
    value_grad = jnp.einsum(
        "sgqk,sqgd->skd",
        prob_vals.astype(jnp.bfloat16),
        do_tiles,
        preferred_element_type=jnp.float32,
    )
    key_grad = (
        jnp.einsum(
            "sgqk,sqgd->skd",
            dscores.astype(jnp.bfloat16),
            q_tiles,
            preferred_element_type=jnp.float32,
        )
        * scale_qk
    )
    key_out = key_grad[:, block_len:] + jnp.concatenate(
        [key_grad[1:, :block_len], jnp.zeros_like(key_grad[:1, :block_len])], 0
    )
    value_out = value_grad[:, block_len:] + jnp.concatenate(
        [value_grad[1:, :block_len], jnp.zeros_like(value_grad[:1, :block_len])], 0
    )
    return (key_out, value_out)


def attend_heads(q_tiles, kv_tiles, do_tiles, stat_tiles, fill_tiles, cont_tiles):
    tile_total, block_len = (q_tiles.shape[0], q_tiles.shape[1])
    kv_cols = kv_tiles.shape[3]
    kv_local = kv_cols // HD
    group_size = q_tiles.shape[2] // kv_cols
    q_heads = q_tiles.reshape(tile_total, block_len, kv_local, group_size, HD)
    do_heads = do_tiles.reshape(tile_total, block_len, kv_local, group_size, HD)
    stat_heads = stat_tiles.reshape(tile_total, block_len, 2, kv_local, group_size)
    results = []
    for head_index in range(kv_local):
        low_col = head_index * HD
        key_out, value_out = band_grads(
            q_heads[:, :, head_index],
            kv_tiles[:, :, 0, low_col : low_col + HD],
            kv_tiles[:, :, 1, low_col : low_col + HD],
            do_heads[:, :, head_index],
            stat_heads[:, :, 0, head_index],
            stat_heads[:, :, 1, head_index],
            fill_tiles,
            cont_tiles,
        )
        results.append(jnp.stack([key_out, value_out], 2))
    return jnp.concatenate(results, 3).astype(jnp.bfloat16)


def per_device(
    layer_input,
    queries,
    keys_values,
    out_grads,
    log_sums,
    deltas,
    tile_fill,
    tile_cont,
    moment_first,
    moment_second,
):
    group_count = lax.axis_size("dp")
    tile_count = tile_fill.shape[1]
    token_count = queries.shape[0]
    block_len = token_count // tile_count
    my_group = lax.axis_index("dp")
    q_tiles = queries.reshape(tile_count, block_len, -1)
    kv_tiles = keys_values.reshape(tile_count, block_len, 2, -1)
    do_tiles = out_grads.reshape(tile_count, block_len, -1)
    stat_tiles = jnp.stack([log_sums, deltas], 1).reshape(tile_count, block_len, 2, -1)
    fill_mine = lax.dynamic_index_in_dim(tile_fill, my_group, 0, keepdims=False)
    cont_mine = lax.dynamic_index_in_dim(tile_cont, my_group, 0, keepdims=False)
    kv_grads = attend_heads(q_tiles, kv_tiles, do_tiles, stat_tiles, fill_mine, cont_mine)
    kv_grads = kv_grads.reshape(token_count, 2, -1)
    terms = jnp.einsum(
        "tr,tkc->rkc",
        layer_input,
        lax.all_gather(kv_grads, "tensor", axis=2, tiled=True),
        preferred_element_type=jnp.float32,
    )
    summed = lax.psum_scatter(terms, "dp", scatter_dimension=0, tiled=True)
    proj_grads = summed / math.sqrt(token_count * group_count)
    new_first = ADAM_ONE * moment_first + (1 - ADAM_ONE) * proj_grads
    heads_kv = moment_second.shape[1]
    partial_squares = jnp.sum(
        jnp.square(proj_grads).reshape(proj_grads.shape[0], 2, heads_kv, -1), axis=(0, 3)
    )
    squares = lax.psum(partial_squares, ("dp", "tensor"))
    new_second = ADAM_TWO * moment_second + (1 - ADAM_TWO) * squares / (D * HD)
    step_size = jnp.sqrt(new_second / (1 - ADAM_TWO**2)) + ADAM_EPS
    scaled = (new_first / (1 - ADAM_ONE**2)).reshape(proj_grads.shape[0], 2, heads_kv, -1)
    update = (scaled / step_size[None, :, :, None]).reshape(proj_grads.shape)
    return (update, new_first, new_second)


def solution(mesh):
    in_specs = (
        P("dp", "tensor"),
        P("dp", "tensor"),
        P("dp", None, "tensor"),
        P("dp", "tensor"),
        P("dp", "tensor"),
        P("dp", "tensor"),
        P(),
        P(),
        P(("tensor", "dp"), None, None),
        P(),
    )
    out_specs = (P(("tensor", "dp"), None, None), P(("tensor", "dp"), None, None), P())
    return jax.shard_map(
        per_device, mesh=mesh, in_specs=in_specs, out_specs=out_specs, check_vma=False
    )
```

profile of v0, /device:TPU:0, one launch (start us, length us, event | category | flops | bytes accessed | tf_op | source)
XLA Modules:
  0.0 350.4 jit_solution(9090283319070825680)
XLA Ops:
  7.2 0.0 copy-start
  7.2 0.0 all-gather.2.cloned.1.call-start
  7.3 1.9 copy.44
  9.1 1.7 slice_bitcast_fusion.2
  10.8 1.7 slice_bitcast_fusion.6
  12.5 0.7 compare_bitcast_fusion
  13.2 0.0 copy-done
  13.2 0.0 copy-start.19
  13.2 0.0 copy-start.20
  13.3 2.6 reshape.151
  15.8 4.0 %reshape.152 = bf16[16,128,2,2,128]{4,3,2,1,0:T(2,128)(2,1)} reshape(bf16[2048,512]{1,0:T(8,128)(2,1)} %param.13) | data formatting | bytes 4194304 | tf_op jit(solution)/shard_map/reshape;reshape | solution.py:70
  19.8 0.0 copy-done.19
  19.8 0.0 copy-done.20
  19.8 0.1 broadcast_and_fusion.1
  19.9 0.1 broadcast_and_fusion
  20.1 0.1 and.20
  20.2 0.0 copy-start.14
  20.2 6.1 %fusion.107 = (bf16[16,128,1,2,128]{4,3,2,1,0:T(2,128)(2,1)S(1)}, bf16[16,128,1,2,128]{4,3,2,1,0:T(2,128)(2,1)}, bf16[16,128,1,2,128]{4,3,2,1,0:T(2,128)(2,1)S(1)}, bf16[16,128,1,2,128]{4,3,2,1,0:T(2,128)(2,1)S(1)}) fusion(bf16[16,128,2,2,128]{4,3,2,1,0:T(2,128)(2,1)} %reshape.152, bf16[16,128,2,2,128]{4,3,2,1,0:T(2,128)(2,1)S(1)} %reshape.151), kind=kLoop, calls=%fused_computation.126 | loop fusion | bytes 8388608 | tf_op jit(solution)/shard_map/slice | solution.py:79
  26.4 0.9 copy-done.4
  27.3 0.0 copy-done.9
  27.3 0.7 fusion.39
  28.1 0.0 copy-start.5
  28.1 0.0 copy-start.17
  28.1 0.0 copy-start.18
  28.1 2.5 fusion.31
  30.6 0.3 copy-done.3
  30.8 0.0 copy-done.17
  30.8 0.2 copy-done.18
  31.1 6.2 %bitcast_multiply_fusion.1 = f32[16,256,128]{2,1,0:T(8,128)} fusion(f32[16,256,128,2]{2,1,3,0:T(8,128)} %copy-done.3, f32[16,2,128]{2,1,0:T(2,128)S(1)} %get-tuple-element.37, f32[16,2,128]{2,1,0:T(2,128)S(1)} %get-tuple-element.35, pred[16,128,256]{1,2,0:T(8,128)(4,1)} %copy-done.14, bf16[15,128,128]{2,1,0:T(8,128)(2,1)S(1)} %copy-done.18, ...), kind=kOutput, calls=%fused_computation.26 | convolution fusion | flops 546832384 | bytes 9961472 | tf_op jit(solution)/shard_map/sgqk,sqgd->skd/dot_general | solution.py:47
  37.3 1.4 slice.129
  38.6 1.4 fusion.59
  40.1 0.2 copy.51
  40.3 0.0 copy-start.11
  40.3 0.7 fusion.47
  41.1 0.5 copy-done.11
  41.5 0.1 copy-done.15
  41.6 2.5 fusion.34
  44.1 0.0 copy-done.2
  44.2 6.1 %bitcast_multiply_fusion = f32[16,256,128]{2,1,0:T(8,128)} fusion(f32[16,256,128,2]{2,1,3,0:T(8,128)} %copy-done.2, f32[16,2,128]{2,1,0:T(2,128)S(1)} %get-tuple-element.36, f32[16,2,128]{2,1,0:T(2,128)S(1)} %get-tuple-element.34, pred[16,128,256]{1,2,0:T(8,128)(4,1)S(1)} %copy-done.16, bf16[15,128,128]{2,1,0:T(8,128)(2,1)} %get-tuple-element.21, ...), kind=kOutput, calls=%fused_computation.25 | convolution fusion | flops 546832384 | bytes 9961472 | tf_op jit(solution)/shard_map/sgqk,sqgd->skd/dot_general | solution.py:47
  50.2 1.3 slice.141
  51.5 1.4 fusion.54
  52.9 0.2 copy.57
  53.2 1.3 slice.131
  54.5 1.4 fusion.58
  55.9 0.2 copy.52
  56.1 1.3 slice.143
  57.4 1.4 fusion.53
  58.8 0.2 copy.58
  59.0 1.5 maximum_maximum_fusion
  60.6 0.0 all-gather.2.cloned.1.call-update
  60.6 0.0 reduce-scatter.2.cloned.1.call-start
  60.7 152.4 %all-gather.2.cloned.1.call-done = bf16[2048,2,1024]{0,2,1:T(8,128)(2,1)} async-done(((bf16[2048,2,256]{0,2,1:T(8,128)(2,1)}), bf16[2048,2,1024]{0,2,1:T(8,128)(2,1)}) %all-gather.2.cloned.1.call-update) | async-done | bytes 8388624 | tf_op jit(solution)/shard_map/all_gather | solution.py:117
  213.1 14.4 %fusion.10 = f32[1024,2,1024]{0,2,1:T(8,128)} fusion(bf16[2048,2,1024]{0,2,1:T(8,128)(2,1)} %all-gather.2.cloned.1.call-done, bf16[2048,1024]{1,0:T(8,128)(2,1)} %param.10), kind=kOutput, calls=%fused_computation.14 | convolution fusion | flops 8589934592 | bytes 20971520 | tf_op jit(solution)/shard_map/tr,tkc->rkc/dot_general | solution.py:114
  227.5 0.0 reduce-scatter.2.cloned.1.call-update
  227.5 69.6 %reduce-scatter.2.cloned.1.call-done = f32[128,2,1024]{0,2,1:T(8,128)} async-done(((f32[1024,2,1024]{0,2,1:T(8,128)}), f32[128,2,1024]{0,2,1:T(8,128)}) %reduce-scatter.2.cloned.1.call-update) | async-done | bytes 1048592 | tf_op jit(solution)/shard_map/reduce_scatter | solution.py:120
  297.1 1.6 multiply_reduce_fusion
  298.7 0.1 bitcast_reduce_fusion
  298.8 0.5 copy.43
  299.3 39.3 %psum.7 = f32[2,8]{1,0:T(2,128)S(1)} all-reduce(f32[2,8]{1,0:T(2,128)S(1)} %bitcast_reduce_fusion), channel_id=1, replica_groups=mesh['dp'=8,'tensor'=4] {'dp','tensor'}, use_global_device_ids=true, to_apply=%region_3.4 | all-reduce | flops 16 | bytes 128 | tf_op jit(solution)/shard_map/psum | solution.py:127
  338.6 0.6 sqrt_add_fusion
  339.2 0.1 broadcast_bitcast_fusion
  339.3 1.6 multiply_divide_fusion
  340.9 1.3 copy.59
  342.2 1.3 copy.60
  (35 shorter events, 0.2 us)
Async XLA Ops:
  7.2 6.1 %copy-start = (s32[8,16]{1,0:T(8,128)S(1)}, s32[8,16]{1,0:T(8,128)}, u32[]{:S(2)}) copy-start(s32[8,16]{1,0:T(8,128)} %param.16) | copy-start | bytes 1540
  7.2 205.9 %all-gather.2.cloned.1.call-start = ((), (), s32[]{:S(2)}) async-start(), calls=%async_computation.1 | async-start | bytes 10485760 | tf_op jit(solution)/shard_map/all_gather | solution.py:117
  13.2 6.6 %copy-start.19 = (bf16[2048,4]{0,1:T(4,128)(2,1)S(1)}, bf16[2048,4]{0,1:T(4,128)(2,1)}, u32[]{:S(2)}) copy-start(bf16[2048,4]{0,1:T(4,128)(2,1)} %param.14) | copy-start | bytes 49156
  13.2 6.6 %copy-start.20 = (bf16[2048,4]{0,1:T(4,128)(2,1)S(1)}, bf16[2048,4]{0,1:T(4,128)(2,1)}, u32[]{:S(2)}) copy-start(bf16[2048,4]{0,1:T(4,128)(2,1)} %param.15) | copy-start | bytes 49156
  20.2 7.9 %copy-start.14 = (pred[16,128,256]{1,2,0:T(8,128)(4,1)}, pred[16,128,256]{1,2,0:T(8,128)(4,1)S(1)}, u32[]{:S(2)}) copy-start(pred[16,128,256]{1,2,0:T(8,128)(4,1)S(1)} %pad_add_fusion) | copy-start | bytes 1572868
  20.2 7.1 %copy-start.7 = (bf16[16,128,128]{2,1,0:T(8,128)(2,1)S(1)}, bf16[16,128,128]{2,1,0:T(8,128)(2,1)}, u32[]{:S(2)}) copy-start(bf16[16,128,128]{2,1,0:T(8,128)(2,1)} %get-tuple-element.19) | copy-start | bytes 1572868
  20.2 7.1 %copy-start.9 = (bf16[15,128,128]{2,1,0:T(8,128)(2,1)S(1)}, bf16[15,128,128]{2,1,0:T(8,128)(2,1)}, u32[]{:S(2)}) copy-start(bf16[15,128,128]{2,1,0:T(8,128)(2,1)} %get-tuple-element.23) | copy-start | bytes 1474564
  26.4 1.0 copy-start.4
  26.4 4.2 %copy-start.13 = (bf16[16,128,1,2,128]{4,3,2,1,0:T(2,128)(2,1)}, bf16[16,128,1,2,128]{4,3,2,1,0:T(2,128)(2,1)S(1)}, u32[]{:S(2)}) copy-start(bf16[16,128,1,2,128]{4,3,2,1,0:T(2,128)(2,1)S(1)} %get-tuple-element.24) | copy-start | bytes 3145732
  28.0 2.8 copy-start.3
  28.1 2.8 copy-start.5
  28.1 2.8 copy-start.17
  28.1 3.0 copy-start.18
  37.3 3.0 copy-start.6
  37.3 3.1 copy-start.8
  40.3 1.2 copy-start.11
  40.3 1.3 copy-start.15
  41.0 3.1 copy-start.2
  41.6 2.5 copy-start.12
  41.6 2.5 copy-start.16
  60.6 236.5 %reduce-scatter.2.cloned.1.call-start = ((), (), s32[]{:S(2)}) async-start(), calls=%async_computation.2 | async-start | bytes 9437184 | tf_op jit(solution)/shard_map/reduce_scatter | solution.py:120
  227.5 71.3 %copy-start.10 = (f32[128,2,1024]{2,1,0:T(2,128)S(1)}, f32[128,2,1024]{2,1,0:T(2,128)}, u32[]{:S(2)}) copy-start(f32[128,2,1024]{2,1,0:T(2,128)} %param.18) | copy-start | bytes 3145732
  227.5 111.1 %copy-start.21 = (f32[2,8]{1,0:T(2,128)S(1)}, f32[2,8]{1,0:T(2,128)}, u32[]{:S(2)}) copy-start(f32[2,8]{1,0:T(2,128)} %param.19) | copy-start | bytes 196
  339.3 4.2 %copy-start.1 = (s32[8,16]{1,0:T(8,128)S(1)}, s32[8,16]{1,0:T(8,128)}, u32[]{:S(2)}) copy-start(s32[8,16]{1,0:T(8,128)} %param.16) | copy-start | bytes 1540
Sparse Core Ops, SparseCore 0:
  60.7 152.3 all-gather.1
  227.6 69.4 reduce-scatter.1
where the time goes:
time: 351 us; the launch traced here: 350 us
  waiting for transfers between devices  222 us (63%)
  blocking collectives  39.3 us (11%)
  matrix products  33 us (9%)
  local copies, waits for them, and re-layouts  29.4 us (8%)
  between operations  14.4 us (4%)
  other arithmetic  12.1 us (3%)
    all_gather x1, waiting for transfers between devices, per_device(): lax.all_gather(kv_grads, 'tensor', axis=2, tiled=True)  152 us
    reduce_scatter x1, waiting for transfers between devices, per_device(): summed = lax.psum_scatter(terms, 'dp', scatter_dimension=0, tiled=True)  69.6 us
    psum x1, blocking collectives, per_device(): squares = lax.psum(partial_squares, ('dp', 'tensor'))  39.3 us
    dot_general x1, matrix products, per_device(): jnp.einsum('tr,tkc->rkc', layer_input, lax.all_gather(kv_grads, 'tensor',...  14.4 us
    dot_general x2, matrix products, band_grads(): jnp.einsum('sgqk,sqgd->skd', dscores.astype(jnp.bfloat16), q_tiles, prefe...  12.3 us
    unnamed x52, local copies, waits for them, and re-layouts  7.17 us
  transfers between devices with their start and end apart: 2, of which 2 were waited for; matrix products, arithmetic and copies ran while one was open for 0% of the time, Pallas kernels for 0%

commit v1 on v0

v1 whole, which is shorter than its diff:
```python
import functools
import math

import jax
import jax.numpy as jnp
from jax import lax
from jax.experimental import pallas as pl
from jax.experimental.pallas import tpu as pltpu
from jax.sharding import PartitionSpec as P

D = 4096
HD = 128

ADAM_ONE = 0.9
ADAM_TWO = 0.95
ADAM_EPS = 1e-08
MESH = pl.DeviceIdType.MESH
NT = (((1,), (1,)), ((), ()))


def attend_kernel(tiles, group_size, fill_ref, cont_ref, q_ref, k_ref, v_ref, do_ref, lse_ref, delta_ref, out_ref):
    group = lax.axis_index("dp")
    block = k_ref.shape[0] // tiles
    scale_qk = HD ** (-0.5)
    wide = 2 * group_size * block
    key_place = lax.broadcasted_iota(jnp.int32, (block, wide), 0)
    column = lax.broadcasted_iota(jnp.int32, (block, wide), 1)
    query_place = column % block
    is_next = column >= group_size * block

    def one_tile(tile, carry):
        after = jnp.minimum(tile + 1, tiles - 1)
        here = pl.ds(pl.multiple_of(tile * block, block), block)
        there = pl.ds(pl.multiple_of(after * block, block), block)
        fill_here = fill_ref[group, tile]
        fill_there = jnp.where(tile + 1 < tiles, fill_ref[group, after] * (cont_ref[group, after] == 1).astype(jnp.int32), 0)
        heads = [slice(h * HD, (h + 1) * HD) for h in range(group_size)]
        q_cat = jnp.concatenate([q_ref[w, h] for w in (here, there) for h in heads], 0)
        do_cat = jnp.concatenate([do_ref[w, h] for w in (here, there) for h in heads], 0)
        lse = jnp.concatenate([lse_ref[0, h : h + 1, w] for w in (here, there) for h in range(group_size)], 1)
        delta = jnp.concatenate([delta_ref[0, h : h + 1, w] for w in (here, there) for h in range(group_size)], 1)
        scores = lax.dot_general(k_ref[here, :], q_cat, NT, preferred_element_type=jnp.float32) * scale_qk
        limit = jnp.where(is_next, fill_there, fill_here)
        allowed = (query_place < limit) & (is_next | (query_place >= key_place))
        prob = jnp.where(allowed, jnp.exp(scores - lse), 0.0)
        dprob = lax.dot_general(v_ref[here, :], do_cat, NT, preferred_element_type=jnp.float32)
        dscore = prob * (dprob - delta)
        value_grad = jnp.dot(prob.astype(jnp.bfloat16), do_cat, preferred_element_type=jnp.float32)
        key_grad = jnp.dot(dscore.astype(jnp.bfloat16), q_cat, preferred_element_type=jnp.float32) * scale_qk
        out_ref[0, here, :] = key_grad.astype(jnp.bfloat16)
        out_ref[1, here, :] = value_grad.astype(jnp.bfloat16)
        return carry

    lax.fori_loop(0, tiles, one_tile, 0, unroll=2)


def attend(queries, keys, values, out_grads, lse_rows, delta_rows, tile_fill, tile_cont):
    tokens = queries.shape[0]
    kv_local = keys.shape[1] // HD
    group_size = queries.shape[1] // keys.shape[1]
    tiles = tile_fill.shape[1]
    smem = pl.BlockSpec(memory_space=pltpu.SMEM)
    q_spec = pl.BlockSpec((tokens, group_size * HD), lambda h: (0, h))
    k_spec = pl.BlockSpec((tokens, HD), lambda h: (0, h))
    row_spec = pl.BlockSpec((1, group_size, tokens), lambda h: (h, 0, 0))
    return pl.pallas_call(
        functools.partial(attend_kernel, tiles, group_size),
        grid=(kv_local,),
        out_shape=jax.ShapeDtypeStruct((2 * kv_local, tokens, HD), jnp.bfloat16),
        in_specs=[smem, smem, q_spec, k_spec, k_spec, q_spec, row_spec, row_spec],
        out_specs=pl.BlockSpec((2, tokens, HD), lambda h: (h, 0, 0)),
        compiler_params=pltpu.CompilerParams(vmem_limit_bytes=32 * 2**20),
    )(tile_fill, tile_cont, queries, keys, values, out_grads, lse_rows, delta_rows)


def sum_kernel(
    groups, planes, inv, kv_ref, layer_ref, out_ref, sq_ref,
    layer, flipped, gathered, terms, pair_send, pair_recv, chip_send, chip_recv, sq_groups, sq_mid, sq_planes,
    load_sem, kv_right, kv_left, kv_recv, pair_ssem, pair_rsem, chip_ssem, chip_rsem,
    sqg_ssem, sqg_rsem, sqp_ssem, sqp_rsem,
):
    me, plane = lax.axis_index("dp"), lax.axis_index("tensor")
    chips = groups // 2
    chip, core = me // 2, me % 2
    partner = me + 1 - 2 * core
    chunks, tokens, _ = kv_ref.shape
    rows = layer_ref.shape[1]
    rows_out = rows // groups

    load = pltpu.make_async_copy(layer_ref, layer, load_sem)
    load.start()

    barrier = pltpu.get_barrier_semaphore()
    for step in range(1, groups):
        pl.semaphore_signal(barrier, inc=1, device_id=(lax.rem(me + step, groups), plane), device_id_type=MESH)
    for step in range(1, planes):
        pl.semaphore_signal(barrier, inc=1, device_id=(me, lax.rem(plane + step, planes)), device_id_type=MESH)
    pl.semaphore_wait(barrier, groups + planes - 2)

    def to_right(source, c, p):
        return pltpu.make_async_remote_copy(
            src_ref=source, dst_ref=gathered.at[c, p], send_sem=kv_right.at[c, p], recv_sem=kv_recv.at[c, p],
            device_id=(me, jnp.minimum(plane + 1, planes - 1)), device_id_type=MESH,
        )

    def to_left(source, c, p):
        return pltpu.make_async_remote_copy(
            src_ref=source, dst_ref=gathered.at[c, p], send_sem=kv_left.at[c, p], recv_sem=kv_recv.at[c, p],
            device_id=(me, jnp.maximum(plane - 1, 0)), device_id_type=MESH,
        )

    def send_own(c):
        @pl.when(plane < planes - 1)
        def _():
            to_right(kv_ref.at[c], c, plane).start()

        @pl.when(plane > 0)
        def _():
            to_left(kv_ref.at[c], c, plane).start()

    row_block = min(256, rows)

    def product(piece_ref, c, p):
        def one(i, carry):
            at = pl.ds(pl.multiple_of(i * row_block, row_block), row_block)
            terms[c, p, at, :] = jnp.dot(flipped[at, :], piece_ref[...], preferred_element_type=jnp.float32)
            return carry

        lax.fori_loop(0, rows // row_block, one, 0)

    def slice_of(k, parity):
        return pl.ds(pl.multiple_of((2 * k + parity) * rows_out, rows_out), rows_out)

    def pair_copy(c):
        return pltpu.make_async_remote_copy(
            src_ref=pair_send.at[c], dst_ref=pair_recv.at[c], send_sem=pair_ssem.at[c], recv_sem=pair_rsem.at[c],
            device_id=(partner, plane), device_id_type=MESH,
        )

    def chip_copy(c, step):
        other = lax.rem(chip + step, chips)
        return pltpu.make_async_remote_copy(
            src_ref=chip_send.at[c, step - 1], dst_ref=chip_recv.at[c, step - 1],
            send_sem=chip_ssem.at[c, step - 1], recv_sem=chip_rsem.at[c, step - 1],
            device_id=(2 * other + core, plane), device_id_type=MESH,
        )

    def stage_one(c):
        for k in range(chips):
            pair_send[c, k] = terms[c, :, slice_of(k, 1 - core), :].astype(jnp.bfloat16)
        pair_copy(c).start()

    def stage_two(c):
        pair_copy(c).wait_recv()
        for step in range(1, chips):
            other = lax.rem(chip + step, chips)
            both = terms[c, :, slice_of(other, core), :] + pair_recv[c, other].astype(jnp.float32)
            chip_send[c, step - 1] = both.astype(jnp.bfloat16)
            chip_copy(c, step).start()

    def stage_three(c):
        total = terms[c, :, slice_of(chip, core), :] + pair_recv[c, chip].astype(jnp.float32)
        for step in range(1, chips):
            chip_copy(c, step).wait_recv()
            total = total + chip_recv[c, step - 1].astype(jnp.float32)
        total = total * inv
        out_ref[c] = total
        squares = jnp.sum(total * total, axis=1)
        sq_groups[me, c] = squares

    send_own(0)
    load.wait()
    flip_block = min(128, rows)

    def flip(i, carry):
        at = pl.ds(pl.multiple_of(i * flip_block, flip_block), flip_block)
        flipped[at, :] = layer[:, at].T
        return carry

    lax.fori_loop(0, rows // flip_block, flip, 0)

    def one_chunk(c, carry):
        product(kv_ref.at[c], c, plane)
        for dist in range(1, planes):
            left, right = plane - dist, plane + dist

            @pl.when(left >= 0)
            def _():
                to_right(kv_ref.at[c], c, left).wait_recv()

                @pl.when(plane < planes - 1)
                def _():
                    to_right(gathered.at[c, left], c, left).start()

            @pl.when(right < planes)
            def _():
                to_left(kv_ref.at[c], c, right).wait_recv()

                @pl.when(plane > 0)
                def _():
                    to_left(gathered.at[c, right], c, right).start()

            if dist == 1:
                @pl.when(c + 1 < chunks)
                def _():
                    send_own(c + 1)

            @pl.when(left >= 0)
            def _():
                product(gathered.at[c, left], c, left)

            @pl.when(right < planes)
            def _():
                product(gathered.at[c, right], c, right)

            if dist == 1:
                @pl.when(c > 0)
                def _():
                    stage_two(c - 1)

            if dist == min(2, planes - 1):
                @pl.when(c > 0)
                def _():
                    stage_three(c - 1)

        stage_one(c)
        return carry

    lax.fori_loop(0, chunks, one_chunk, 0)
    stage_two(chunks - 1)
    stage_three(chunks - 1)

    def sq_group_copy(step):
        return pltpu.make_async_remote_copy(
            src_ref=sq_groups.at[me], dst_ref=sq_groups.at[me], send_sem=sqg_ssem.at[step - 1],
            recv_sem=sqg_rsem.at[step - 1],
            device_id=(lax.rem(me + step, groups), plane), device_id_type=MESH,
        )

    for step in range(1, groups):
        sq_group_copy(step).start()
    for step in range(1, groups):
        sq_group_copy(step).wait_recv()
    sq_mid[...] = sq_groups[0]
    for g in range(1, groups):
        sq_mid[...] += sq_groups[g]
    sq_planes[plane] = sq_mid[...]

    def sq_plane_copy(step):
        return pltpu.make_async_remote_copy(
            src_ref=sq_mid, dst_ref=sq_planes.at[plane], send_sem=sqp_ssem.at[step - 1],
            recv_sem=sqp_rsem.at[step - 1],
            device_id=(me, lax.rem(plane + step, planes)), device_id_type=MESH,
        )

    for step in range(1, planes):
        sq_plane_copy(step).start()
    for step in range(1, planes):
        sq_plane_copy(step).wait_recv()
    summed = sq_planes[0]
    for p in range(1, planes):
        summed = summed + sq_planes[p]
    sq_ref[...] = summed

    for step in range(1, groups):
        sq_group_copy(step).wait_send()
    for step in range(1, planes):
        sq_plane_copy(step).wait_send()

    def drain(c, carry):
        pair_copy(c).wait_send()
        for step in range(1, chips):
            chip_copy(c, step).wait_send()
        for p in range(planes):
            @pl.when((plane < planes - 1) & (p <= plane))
            def _():
                to_right(kv_ref.at[c], c, p).wait_send()

            @pl.when((plane > 0) & (p >= plane))
            def _():
                to_left(kv_ref.at[c], c, p).wait_send()
        return carry

    lax.fori_loop(0, chunks, drain, 0)


def sum_over_groups(kv_chunks, layer_input, groups, planes):
    chunks, tokens, _ = kv_chunks.shape
    rows = layer_input.shape[1]
    rows_out = rows // groups
    chips = groups // 2
    half, full = jnp.bfloat16, jnp.float32
    dma = pltpu.SemaphoreType.DMA
    vmem = pl.BlockSpec(memory_space=pltpu.VMEM)
    return pl.pallas_call(
        functools.partial(sum_kernel, groups, planes, 1.0 / math.sqrt(tokens * groups)),
        out_shape=(
            jax.ShapeDtypeStruct((chunks, planes, rows_out, HD), full),
            jax.ShapeDtypeStruct((chunks, planes, HD), full),
        ),
        in_specs=[vmem, pl.BlockSpec(memory_space=pl.ANY)],
        out_specs=(vmem, vmem),
        scratch_shapes=[
            pltpu.VMEM((tokens, rows), half),
            pltpu.VMEM((rows, tokens), half),
            pltpu.VMEM((chunks, planes, tokens, HD), half),
            pltpu.VMEM((chunks, planes, rows, HD), full),
            pltpu.VMEM((chunks, chips, planes, rows_out, HD), half),
            pltpu.VMEM((chunks, chips, planes, rows_out, HD), half),
            pltpu.VMEM((chunks, chips - 1, planes, rows_out, HD), half),
            pltpu.VMEM((chunks, chips - 1, planes, rows_out, HD), half),
            pltpu.VMEM((groups, chunks, planes, HD), full),
            pltpu.VMEM((chunks, planes, HD), full),
            pltpu.VMEM((planes, chunks, planes, HD), full),
            dma,
            dma((chunks, planes)),
            dma((chunks, planes)),
            dma((chunks, planes)),
            dma((chunks,)),
            dma((chunks,)),
            dma((chunks, chips - 1)),
            dma((chunks, chips - 1)),
            dma((groups - 1,)),
            dma((groups - 1,)),
            dma((planes - 1,)),
            dma((planes - 1,)),
        ],
        compiler_params=pltpu.CompilerParams(
            collective_id=0, has_side_effects=True, vmem_limit_bytes=56 * 2**20
        ),
    )(kv_chunks, layer_input)


def per_device(
    layer_input, queries, keys_values, out_grads, log_sums, deltas, tile_fill, tile_cont, moment_first, moment_second
):
    groups, planes = lax.axis_size("dp"), lax.axis_size("tensor")
    keys, values = keys_values[:, 0], keys_values[:, 1]
    tokens = queries.shape[0]
    kv_local = keys.shape[1] // HD
    lse_rows = log_sums.astype(jnp.float32).T.reshape(kv_local, -1, tokens)
    delta_rows = deltas.astype(jnp.float32).T.reshape(kv_local, -1, tokens)
    kv_chunks = attend(queries, keys, values, out_grads, lse_rows, delta_rows, tile_fill, tile_cont)
    summed, lane_squares = sum_over_groups(kv_chunks, layer_input, groups, planes)
    rows_out = summed.shape[2]
    heads_kv = moment_second.shape[1]
    parts = summed.reshape(kv_local, 2, planes, rows_out, HD)
    proj_grads = parts.transpose(3, 1, 2, 0, 4).reshape(rows_out, 2, -1)
    squares = jnp.sum(lane_squares.reshape(kv_local, 2, planes, HD), 3).transpose(1, 2, 0).reshape(2, heads_kv)
    new_first = ADAM_ONE * moment_first + (1 - ADAM_ONE) * proj_grads
    new_second = ADAM_TWO * moment_second + (1 - ADAM_TWO) * squares / (D * HD)
    step_size = jnp.sqrt(new_second / (1 - ADAM_TWO**2)) + ADAM_EPS
    scaled = (new_first / (1 - ADAM_ONE**2)).reshape(rows_out, 2, heads_kv, -1)
    update = (scaled / step_size[None, :, :, None]).reshape(proj_grads.shape)
    return (update, new_first, new_second)


def solution(mesh):
    in_specs = (
        P("dp", "tensor"),
        P("dp", "tensor"),
        P("dp", None, "tensor"),
        P("dp", "tensor"),
        P("dp", "tensor"),
        P("dp", "tensor"),
        P(),
        P(),
        P(("tensor", "dp"), None, None),
        P(),
    )
    out_specs = (P(("tensor", "dp"), None, None), P(("tensor", "dp"), None, None), P())
    return jax.shard_map(
        per_device, mesh=mesh, in_specs=in_specs, out_specs=out_specs, check_vma=False
    )
```

time: 351 us -> 193 us (0.55)
  waiting for transfers between devices: 222 us -> 0 us
  Pallas kernels: 0 us -> 174 us
  blocking collectives: 39.3 us -> 0 us
  matrix products: 33 us -> 0 us
  local copies, waits for them, and re-layouts: 29.4 us -> 13.1 us
  between operations: 14.4 us -> 0.79 us
  other arithmetic: 12.1 us -> 5.09 us
    pallas_call x0 -> x2, Pallas kernels: none -> 174 us  [the longest x1 163 us: sum_over_groups(): pl.pallas_call(functools.partial(sum_kernel, groups, planes, 1.0 / math.s...]
    all_gather x1 -> x0, waiting for transfers between devices: 152 us -> none  [per_device(): lax.all_gather(kv_grads, 'tensor', axis=2, tiled=True)]
    reduce_scatter x1 -> x0, waiting for transfers between devices: 69.6 us -> none  [per_device(): summed = lax.psum_scatter(terms, 'dp', scatter_dimension=0, tiled=True)]
    psum x1 -> x0, blocking collectives: 39.3 us -> none  [per_device(): squares = lax.psum(partial_squares, ('dp', 'tensor'))]
    dot_general x7 -> x0, matrix products: 33 us -> none  [the longest x1 14.4 us: per_device(): jnp.einsum('tr,tkc->rkc', layer_input, lax.all_gather(kv_grads, 'tensor',...]
    another operation x6 -> x0, local copies, waits for them, and re-layouts: 7.43 us -> none  [the longest x1 3.97 us: attend_heads(): do_heads = do_tiles.reshape(tile_total, block_len, kv_local, group_size, HD)]
    slice x6 -> x1, local copies, waits for them, and re-layouts: 13 us -> 5.55 us  [per_device(): keys, values = (keys_values[:, 0], keys_values[:, 1])]
    another operation x4 -> x0, other arithmetic: 5.7 us -> none
  transfers between devices with their start and end apart: 2 -> 0, of which waited for: 2 -> 0; matrix products, arithmetic and copies ran while one was open for 0% -> 0% of each run, Pallas kernels for 0% -> 0%
where the time goes in v1:
time: 193 us
  Pallas kernels  174 us (90%)
  local copies, waits for them, and re-layouts  13.1 us (7%)
  other arithmetic  5.09 us (3%)
    pallas_call x1, Pallas kernels, sum_over_groups(): pl.pallas_call(functools.partial(sum_kernel, groups, planes, 1.0 / math.s...  163 us
    pallas_call x1, Pallas kernels, attend(): pl.pallas_call(functools.partial(attend_kernel, tiles, group_size), grid=...  11 us
    slice x1, local copies, waits for them, and re-layouts, per_device(): keys, values = (keys_values[:, 0], keys_values[:, 1])  5.55 us
    unnamed x20, local copies, waits for them, and re-layouts  4.83 us

profile of v1, /device:TPU:0, one launch (start us, length us, event | category | flops | bytes accessed | tf_op | source)
XLA Modules:
  0.0 192.8 jit_solution(15414848760976079674)
XLA Ops:
  0.6 5.6 %fusion = (bf16[2048,1,256]{2,1,0:T(2,128)(2,1)S(1)}, bf16[2048,1,256]{2,1,0:T(2,128)(2,1)S(1)}) fusion(bf16[2048,2,256]{2,1,0:T(2,128)(2,1)} %param.12), kind=kLoop, calls=%fused_computation.12 | loop fusion | bytes 4194304 | tf_op jit(solution)/shard_map/slice | solution.py:338
  6.2 0.0 copy-start.6
  6.2 0.0 copy-start.7
  6.2 0.0 copy-start.3
  6.2 0.0 copy-start.4
  6.2 0.5 copy_bitcast_fusion
  6.7 0.2 copy-done.6
  7.0 0.0 copy-done.7
  7.0 0.0 copy-done.3
  7.0 0.0 copy-done.4
  7.0 0.0 copy-start.1
  7.0 1.6 copy-done.1
  8.6 0.0 copy-start.2
  8.6 1.6 copy-done.2
  10.2 11.0 %shard_map.121.kv_ref = bf16[4,2048,128]{2,1,0:T(8,128)(2,1)S(1)} custom-call(s32[8,16]{1,0:T(8,128)S(1)} %copy-done.3, s32[8,16]{1,0:T(8,128)S(1)} %copy-done.4, bf16[2048,512]{1,0:T(8,128)(2,1)S(1)} %copy-done.1, bf16[2048,256]{1,0:T(8,128)(2,1)S(1)} %get-tuple-element.14.k_ref, bf16[2048,256]{1,0:T(8,128)(2,1)S(1)} %get-tuple-element.13.v_ref, ...), custom_call_target="tpu_custom_call" | custom-call | tf_op jit(solution)/shard_map/pallas_call | solution.py:66
  21.2 0.0 copy-start
  21.2 1.3 copy-done
  22.5 0.0 copy-start.8
  22.5 162.9 %shard_map.122 = (f32[4,4,128,128]{3,2,1,0:T(8,128)}, f32[4,4,128]{2,1,0:T(4,128)}) custom-call(bf16[4,2048,128]{2,1,0:T(8,128)(2,1)} %copy-done, bf16[2048,1024]{1,0:T(8,128)(2,1)} %layer_ref.1), custom_call_target="tpu_custom_call" | custom-call | tf_op jit(solution)/shard_map/pallas_call | solution.py:295
  185.4 0.8 reduce_sum.9
  186.2 0.1 copy.20
  186.3 0.1 div.39
  186.4 0.0 copy-done.8
  186.4 0.6 sqrt_add_fusion
  187.0 0.1 broadcast_bitcast_fusion
  187.1 1.3 broadcast_multiply_fusion
  188.4 0.0 copy-start.5
  188.4 0.8 copy.19
  189.2 1.2 mul.31
  190.4 0.0 copy-done.5
  190.4 2.4 %multiply_divide_fusion = (f32[128,2,1024]{2,1,0:T(2,128)}, f32[128,2,1024]{2,1,0:T(2,128)}) fusion(f32[2,1024]{1,0:T(2,128)S(1)} %bitcast.20, f32[128,2,1024]{2,1,0:T(2,128)S(1)} %mul.31, f32[128,2,1024]{2,1,0:T(2,128)S(1)} %copy-done.5), kind=kLoop, calls=%fused_computation.2 | loop fusion | flops 1048576 | bytes 4202496 | tf_op jit(solution)/shard_map/div | solution.py:354
  (6 shorter events, 0.1 us)
Async XLA Ops:
  6.2 0.7 copy-start.6
  6.2 0.8 copy-start.7
  6.2 0.8 copy-start.3
  6.2 0.8 copy-start.4
  7.0 1.6 copy-start.1
  8.6 1.6 copy-start.2
  21.2 1.3 copy-start
  22.5 163.9 %copy-start.8 = (f32[2,8]{1,0:T(2,128)S(1)}, f32[2,8]{1,0:T(2,128)}, u32[]{:S(2)}) copy-start(f32[2,8]{1,0:T(2,128)} %param.19) | copy-start | bytes 196
  188.4 2.0 %copy-start.5 = (f32[128,2,1024]{2,1,0:T(2,128)S(1)}, f32[128,2,1024]{2,1,0:T(2,128)}, u32[]{:S(2)}) copy-start(f32[128,2,1024]{2,1,0:T(2,128)} %param.18) | copy-start | bytes 3145732
